TPU v7x, 32 devices: a whole 2x2x4 slice. The times are simulated.
32 devices in a mesh: seq: 16 (over z, y, core), head: 2 (over x).
Axes of the slice: x: 2, y: 2, z: 4, core: 2. Of those that a mesh axis runs over, the one named last changes fastest.
Arguments:
- queries: bfloat16 [256, 64, 128], P('seq', 'head'), may hold values from -5 to 5
- cache: bfloat16 [2, 1024, 8, 128, 128], P(None, 'seq', 'head'), may hold values from -5 to 5
- page_table: int32 [256, 64], replicated, may hold values from 0 to 1023, as said below
- page_count: int32 [256], replicated, may hold values from 32 to 64, as said below
- out_weight: bfloat16 [8192, 8192], P('head', 'seq'), may hold values from -0.0625 to 0.0625
Outputs:
- output: bfloat16 [256, 8192], P('head', 'seq')
Inputs may be any that keep to these rules, and one draw needn't show every extreme that they name: `page_table`: within a row all 64 entries are distinct page ids; only the first page_count entries of a row are selected, the rest are arbitrary. In every row at most 4 entries lie in one aligned block of 64 page ids, and the first 4 entries of every row lie in one such block. `page_count`: some sequence has exactly 64 selected pages.
All inputs are finite; a program needn't handle non-finite values.
Results may differ from a plain program's by a relative error of at most 0.0095.
Values may be sent and summed in bfloat16 or wider, within the bound.
No kernel may reach another device: no remote copies, remote signals or barrier semaphores. Data moves between devices by JAX's collectives and lax.ppermute only.
A program may use at most 192 MiB of HBM per device.

v0:
```python
import math
import jax
import jax.numpy as jnp
from jax import lax
from jax.sharding import PartitionSpec as P

CAP = 4


def shards(queries, cache, page_table, page_count, out_weight):
    own_index = lax.axis_index("seq")
    key_pages = cache[0]
    value_pages = cache[1]
    pages_here = key_pages.shape[0]
    kv_local = key_pages.shape[1]
    query_heads = queries.shape[1]
    head_dim = queries.shape[2]
    group_size = query_heads // kv_local
    score_scale = 1.0 / math.sqrt(head_dim)

    def local_pages(selected, counts):
        slots = selected.shape[1]
        position = jnp.arange(slots, dtype=jnp.int32)
        usable = position[None, :] < counts[:, None]
        present = usable & (selected // pages_here == own_index)
        upper = (position[:, None] <= position[None, :]).astype(jnp.float32)
        ranks = jnp.dot(present.astype(jnp.float32), upper).astype(jnp.int32) - 1
        target = jnp.arange(CAP, dtype=jnp.int32)[None, :, None]
        onehot = present[:, None, :] & (ranks[:, None, :] == target)
        picked = jnp.sum(jnp.where(onehot, selected[:, None, :], 0), axis=2)
        valid = jnp.any(onehot, axis=2)
        index = jnp.where(valid, picked - own_index * pages_here, 0)
        return (index, valid)

    def block_scores(query_block, index, valid):
        block_rows = query_block.shape[0]
        grouped = query_block.reshape(block_rows, kv_local, group_size, head_dim)
        keys = key_pages[index]
        scores = (
            jnp.einsum("skgd,scktd->skgct", grouped, keys, preferred_element_type=jnp.float32)
            * score_scale
        )
        allowed = valid[:, None, None, :, None]
        return jnp.where(allowed, scores, jnp.float32(-1e30))

    def weigh_block(scores, index, valid, maxima):
        allowed = valid[:, None, None, :, None]
        weights = jnp.where(allowed, jnp.exp(scores - maxima[..., None, None]), jnp.float32(0.0))
        totals = jnp.sum(weights, axis=(3, 4))
        values = value_pages[index]
        update = jnp.einsum(
            "skgct,scktd->skgd",
            weights.astype(jnp.bfloat16),
            values,
            preferred_element_type=jnp.float32,
        )
        return (totals, update)

    all_queries = lax.all_gather(queries, "seq", axis=0, tiled=True)
    batch_rows = all_queries.shape[0]
    block_size = math.gcd(batch_rows, 64)
    blocks = batch_rows // block_size
    query_blocks = all_queries.reshape(blocks, block_size, query_heads, head_dim)
    table_blocks = page_table.reshape(blocks, block_size, page_table.shape[1])
    count_blocks = page_count.reshape(blocks, block_size)

    def score_many(inputs):
        query_block, selected, counts = inputs
        index, valid = local_pages(selected, counts)
        scores = block_scores(query_block, index, valid)
        return (scores, index, valid, jnp.max(scores, axis=(3, 4)))

    scores, index, valid, maxima = lax.map(score_many, (query_blocks, table_blocks, count_blocks))
    largest = lax.pmax(maxima, "seq")

    def weigh_many(inputs):
        block_scores_now, block_index, block_valid, block_largest = inputs
        return weigh_block(block_scores_now, block_index, block_valid, block_largest)

    totals, outputs = lax.map(weigh_many, (scores, index, valid, largest))
    totals = totals.reshape(batch_rows, kv_local, group_size)
    outputs = outputs.reshape(batch_rows, kv_local, group_size, head_dim)
    summed_outputs, summed_totals = lax.psum((outputs, totals), "seq")
    attention = (
        (summed_outputs / summed_totals[..., None])
        .reshape(batch_rows, query_heads * head_dim)
        .astype(jnp.bfloat16)
    )
    picked = attention
    summed = lax.psum_scatter(
        jnp.dot(picked, out_weight, preferred_element_type=jnp.float32),
        "head",
        scatter_dimension=0,
        tiled=True,
    )
    return summed.astype(jnp.bfloat16)


def solution(mesh):
    return jax.shard_map(
        shards,
        mesh=mesh,
        in_specs=(
            P("seq", "head", None),
            P(None, "seq", "head", None, None),
            P(),
            P(),
            P("head", "seq"),
        ),
        out_specs=P("head", "seq"),
        check_vma=False,
    )
```

profile of v0, /device:TPU:0, one launch (start us, length us, event | category | flops | bytes accessed | tf_op | source)
XLA Modules:
  0.0 540.8 jit_solution(4979630972835469058)
XLA Ops:
  6.5 0.7 all-gather.2.cloned.1.call-update
  7.3 0.9 copy.26
  8.3 0.8 reshape.191
  9.1 11.9 %slice_bitcast_fusion = (bf16[64,4,128,128]{3,2,1,0:T(8,128)(2,1)}, bf16[64,4,128,128]{3,2,1,0:T(8,128)(2,1)}) fusion(bf16[2,64,4,128,128]{4,3,2,1,0:T(8,128)(2,1)} %param.10), kind=kLoop, calls=%fused_computation.56 | loop fusion | bytes 33554432 | tf_op jit(solution)/shard_map/squeeze | solution.py:13
  21.0 32.8 %all-gather.2.cloned.1.call-done = bf16[256,32,128]{2,1,0:T(8,128)(2,1)} async-done(((bf16[16,32,128]{2,1,0:T(8,128)(2,1)}), bf16[256,32,128]{2,1,0:T(8,128)(2,1)}) %all-gather.2.cloned.1.call-update) | async-done | bytes 2097168 | tf_op jit(solution)/shard_map/all_gather | solution.py:59
  53.8 142.4 %while.31 = (s32[]{:T(128)}, f32[4,64,4,8,4,128]{5,3,4,2,1,0:T(8,128)}, s32[4,64,4]{1,2,0:T(4,128)S(1)}, pred[4,64,4]{1,2,0:T(4,128)(4,1)S(1)}, f32[4,64,4,8]{3,...) while((s32[]{:T(128)}, ...), condition=%wide.region_4.5_spmd, body=%wide.region_0.4_spmd.sunk | while | flops 274403584 | bytes 114177944 | solution.py:73
  54.0 0.1 select_reduce_fusion.2
  54.2 0.2 fusion.57
  54.6 17.1 %gather_fusion.1 = bf16[256,4,128,128]{3,2,1,0:T(8,128)(2,1)} fusion(bf16[64,4,128,128]{3,2,1,0:T(8,128)(2,1)} %get-tuple-element.437, s32[1024]{0:T(1024)S(1)} %pad_clamp_fusion.4), kind=kCustom, calls=%fused_computation.clone.1 | custom fusion | bytes 67109888 | tf_op jit(solution)/shard_map/while/body/eval_jaxpr/gather | solution.py:38
  71.8 16.0 %bitcast_dynamic-update-slice_fusion.8 = (f32[4,64,4,8,4,128]{5,3,4,2,1,0:T(8,128)}, f32[64,4,8,4,128]{4,2,3,1,0:T(8,128)S(1)}) fusion(f32[4,64,4,8,4,128]{5,3,4,2,1,0:T(8,128)} %get-tuple-element.416, s32[]{:T(128)} %get-tuple-element.415, pred[64,4]{1,0:T(8,128)(4,1)S(1)} %copy.58, bf16[64,4,4,128,128]{4,3,2,1,0:T(8,128)(2,1)} %bitcast.114, ...), kind=kOutput, calls=%fused_computation.4.clone.1 | convolution fusion | flops 270532608 | bytes 42468608 | tf_op jit(solution)/shard_map/while/body/eval_jaxpr/skgd,scktd->skgct/dot_general | solution.py:40
  87.8 1.5 fusion.59
  89.6 0.1 select_reduce_fusion.2
  89.8 0.2 fusion.57
  90.2 17.1 %gather_fusion.1 = bf16[256,4,128,128]{3,2,1,0:T(8,128)(2,1)} fusion(bf16[64,4,128,128]{3,2,1,0:T(8,128)(2,1)} %get-tuple-element.437, s32[1024]{0:T(1024)S(1)} %pad_clamp_fusion.4), kind=kCustom, calls=%fused_computation.clone.1 | custom fusion | bytes 67109888 | tf_op jit(solution)/shard_map/while/body/eval_jaxpr/gather | solution.py:38
  107.4 16.0 %bitcast_dynamic-update-slice_fusion.8 = (f32[4,64,4,8,4,128]{5,3,4,2,1,0:T(8,128)}, f32[64,4,8,4,128]{4,2,3,1,0:T(8,128)S(1)}) fusion(f32[4,64,4,8,4,128]{5,3,4,2,1,0:T(8,128)} %get-tuple-element.416, s32[]{:T(128)} %get-tuple-element.415, pred[64,4]{1,0:T(8,128)(4,1)S(1)} %copy.58, bf16[64,4,4,128,128]{4,3,2,1,0:T(8,128)(2,1)} %bitcast.114, ...), kind=kOutput, calls=%fused_computation.4.clone.1 | convolution fusion | flops 270532608 | bytes 42468608 | tf_op jit(solution)/shard_map/while/body/eval_jaxpr/skgd,scktd->skgct/dot_general | solution.py:40
  123.4 1.5 fusion.59
  125.4 0.2 fusion.57
  125.8 17.1 %gather_fusion.1 = bf16[256,4,128,128]{3,2,1,0:T(8,128)(2,1)} fusion(bf16[64,4,128,128]{3,2,1,0:T(8,128)(2,1)} %get-tuple-element.437, s32[1024]{0:T(1024)S(1)} %pad_clamp_fusion.4), kind=kCustom, calls=%fused_computation.clone.1 | custom fusion | bytes 67109888 | tf_op jit(solution)/shard_map/while/body/eval_jaxpr/gather | solution.py:38
  143.0 15.9 %bitcast_dynamic-update-slice_fusion.8 = (f32[4,64,4,8,4,128]{5,3,4,2,1,0:T(8,128)}, f32[64,4,8,4,128]{4,2,3,1,0:T(8,128)S(1)}) fusion(f32[4,64,4,8,4,128]{5,3,4,2,1,0:T(8,128)} %get-tuple-element.416, s32[]{:T(128)} %get-tuple-element.415, pred[64,4]{1,0:T(8,128)(4,1)S(1)} %copy.58, bf16[64,4,4,128,128]{4,3,2,1,0:T(8,128)(2,1)} %bitcast.114, ...), kind=kOutput, calls=%fused_computation.4.clone.1 | convolution fusion | flops 270532608 | bytes 42468608 | tf_op jit(solution)/shard_map/while/body/eval_jaxpr/skgd,scktd->skgct/dot_general | solution.py:40
  158.9 1.5 fusion.59
  160.8 0.1 select_reduce_fusion.2
  161.0 0.2 fusion.57
  161.4 17.1 %gather_fusion.1 = bf16[256,4,128,128]{3,2,1,0:T(8,128)(2,1)} fusion(bf16[64,4,128,128]{3,2,1,0:T(8,128)(2,1)} %get-tuple-element.437, s32[1024]{0:T(1024)S(1)} %pad_clamp_fusion.4), kind=kCustom, calls=%fused_computation.clone.1 | custom fusion | bytes 67109888 | tf_op jit(solution)/shard_map/while/body/eval_jaxpr/gather | solution.py:38
  178.6 16.0 %bitcast_dynamic-update-slice_fusion.8 = (f32[4,64,4,8,4,128]{5,3,4,2,1,0:T(8,128)}, f32[64,4,8,4,128]{4,2,3,1,0:T(8,128)S(1)}) fusion(f32[4,64,4,8,4,128]{5,3,4,2,1,0:T(8,128)} %get-tuple-element.416, s32[]{:T(128)} %get-tuple-element.415, pred[64,4]{1,0:T(8,128)(4,1)S(1)} %copy.58, bf16[64,4,4,128,128]{4,3,2,1,0:T(8,128)(2,1)} %bitcast.114, ...), kind=kOutput, calls=%fused_computation.4.clone.1 | convolution fusion | flops 270532608 | bytes 42468608 | tf_op jit(solution)/shard_map/while/body/eval_jaxpr/skgd,scktd->skgct/dot_general | solution.py:40
  194.5 1.5 fusion.59
  196.2 64.9 %pmax.7 = f32[4,64,4,8]{3,2,1,0:T(4,128)S(1)} all-reduce(f32[4,64,4,8]{3,2,1,0:T(4,128)S(1)} %get-tuple-element.215), channel_id=1, replica_groups=mesh['seq'=16,'head'=2] {'seq'}, use_global_device_ids=true, to_apply=%region_5.6 | all-reduce | flops 8192 | bytes 65536 | tf_op jit(solution)/shard_map/pmax | solution.py:74
  261.1 143.1 %while.32 = (s32[]{:T(128)}, f32[4,64,4,8]{3,2,1,0:T(4,128)S(1)}, f32[4,64,4,8,128]{4,3,2,1,0:T(8,128)}, pred[4,64,4]{1,2,0:T(4,128)(4,1)S(1)}, f32[4,64,4,8,4,1...) while((s32[]{:T(128)}, f32[4,64,4,8]{3,2,1,0:T(4,128)S(1)}, ...), condition=%wide.region_8.9_spmd, body=%wide.region_6.8_spmd.sunk | while | flops 274726656 | bytes 110420592 | solution.py:80
  261.4 17.1 %gather_fusion = bf16[256,4,128,128]{3,2,1,0:T(8,128)(2,1)} fusion(bf16[64,4,128,128]{3,2,1,0:T(8,128)(2,1)} %get-tuple-element.464, s32[1024]{0:T(1024)S(1)} %pad_clamp_fusion.5), kind=kCustom, calls=%fused_computation.1.clone.1 | custom fusion | bytes 67109888 | tf_op jit(solution)/shard_map/while/body/eval_jaxpr/gather | solution.py:50
  278.6 15.2 %fusion.63 = f32[4,64,4,8,128]{4,3,2,1,0:T(8,128)} fusion(f32[4,64,4,8,128]{4,3,2,1,0:T(8,128)} %get-tuple-element.450, s32[]{:T(128)} %get-tuple-element.448, bf16[64,4,4,128,128]{4,3,2,1,0:T(8,128)(2,1)} %bitcast.115, f32[4,64,4,8,4,128]{5,3,4,2,1,0:T(8,128)} %get-tuple-element.461, f32[64,4,8]{2,1,0:T(4,128)S(1)} %dynamic-slice_bitcast_fusion.4, ...), kind=kOutput, calls=%fused_computation.47.clone.1 | convolution fusion | flops 271581184 | bytes 38806784 | tf_op jit(solution)/shard_map/while/body/eval_jaxpr/skgct,scktd->skgd/dot_general | solution.py:51
  293.8 3.1 fusion.62
  297.1 17.1 %gather_fusion = bf16[256,4,128,128]{3,2,1,0:T(8,128)(2,1)} fusion(bf16[64,4,128,128]{3,2,1,0:T(8,128)(2,1)} %get-tuple-element.464, s32[1024]{0:T(1024)S(1)} %pad_clamp_fusion.5), kind=kCustom, calls=%fused_computation.1.clone.1 | custom fusion | bytes 67109888 | tf_op jit(solution)/shard_map/while/body/eval_jaxpr/gather | solution.py:50
  314.3 15.2 %fusion.63 = f32[4,64,4,8,128]{4,3,2,1,0:T(8,128)} fusion(f32[4,64,4,8,128]{4,3,2,1,0:T(8,128)} %get-tuple-element.450, s32[]{:T(128)} %get-tuple-element.448, bf16[64,4,4,128,128]{4,3,2,1,0:T(8,128)(2,1)} %bitcast.115, f32[4,64,4,8,4,128]{5,3,4,2,1,0:T(8,128)} %get-tuple-element.461, f32[64,4,8]{2,1,0:T(4,128)S(1)} %dynamic-slice_bitcast_fusion.4, ...), kind=kOutput, calls=%fused_computation.47.clone.1 | convolution fusion | flops 271581184 | bytes 38806784 | tf_op jit(solution)/shard_map/while/body/eval_jaxpr/skgct,scktd->skgd/dot_general | solution.py:51
  329.5 3.1 fusion.62
  332.9 17.1 %gather_fusion = bf16[256,4,128,128]{3,2,1,0:T(8,128)(2,1)} fusion(bf16[64,4,128,128]{3,2,1,0:T(8,128)(2,1)} %get-tuple-element.464, s32[1024]{0:T(1024)S(1)} %pad_clamp_fusion.5), kind=kCustom, calls=%fused_computation.1.clone.1 | custom fusion | bytes 67109888 | tf_op jit(solution)/shard_map/while/body/eval_jaxpr/gather | solution.py:50
  350.2 15.2 %fusion.63 = f32[4,64,4,8,128]{4,3,2,1,0:T(8,128)} fusion(f32[4,64,4,8,128]{4,3,2,1,0:T(8,128)} %get-tuple-element.450, s32[]{:T(128)} %get-tuple-element.448, bf16[64,4,4,128,128]{4,3,2,1,0:T(8,128)(2,1)} %bitcast.115, f32[4,64,4,8,4,128]{5,3,4,2,1,0:T(8,128)} %get-tuple-element.461, f32[64,4,8]{2,1,0:T(4,128)S(1)} %dynamic-slice_bitcast_fusion.4, ...), kind=kOutput, calls=%fused_computation.47.clone.1 | convolution fusion | flops 271581184 | bytes 38806784 | tf_op jit(solution)/shard_map/while/body/eval_jaxpr/skgct,scktd->skgd/dot_general | solution.py:51
  365.4 3.1 fusion.62
  368.7 17.1 %gather_fusion = bf16[256,4,128,128]{3,2,1,0:T(8,128)(2,1)} fusion(bf16[64,4,128,128]{3,2,1,0:T(8,128)(2,1)} %get-tuple-element.464, s32[1024]{0:T(1024)S(1)} %pad_clamp_fusion.5), kind=kCustom, calls=%fused_computation.1.clone.1 | custom fusion | bytes 67109888 | tf_op jit(solution)/shard_map/while/body/eval_jaxpr/gather | solution.py:50
  385.9 15.2 %fusion.63 = f32[4,64,4,8,128]{4,3,2,1,0:T(8,128)} fusion(f32[4,64,4,8,128]{4,3,2,1,0:T(8,128)} %get-tuple-element.450, s32[]{:T(128)} %get-tuple-element.448, bf16[64,4,4,128,128]{4,3,2,1,0:T(8,128)(2,1)} %bitcast.115, f32[4,64,4,8,4,128]{5,3,4,2,1,0:T(8,128)} %get-tuple-element.461, f32[64,4,8]{2,1,0:T(4,128)S(1)} %dynamic-slice_bitcast_fusion.4, ...), kind=kOutput, calls=%fused_computation.47.clone.1 | convolution fusion | flops 271581184 | bytes 38806784 | tf_op jit(solution)/shard_map/while/body/eval_jaxpr/skgct,scktd->skgd/dot_general | solution.py:51
  401.1 3.1 fusion.62
  404.3 0.2 copy.33
  404.5 58.7 %psum.15 = f32[256,4,8]{0,2,1:T(8,128)S(1)} all-reduce(f32[256,4,8]{0,2,1:T(8,128)S(1)} %copy.33), channel_id=1, replica_groups=mesh['seq'=16,'head'=2] {'seq'}, use_global_device_ids=true, to_apply=%region_10.11 | all-reduce | flops 8192 | bytes 65536 | tf_op jit(solution)/shard_map/psum | solution.py:83
  463.2 0.2 copy.30
  463.4 49.9 %all-reduce.2.cloned.1.call-done = f32[256,4,8,128]{3,2,1,0:T(8,128)} async-done(((f32[256,4,8,128]{3,2,1,0:T(8,128)}), f32[256,4,8,128]{3,2,1,0:T(8,128)}) %all-reduce.2.cloned.1.call-update) | async-done | bytes 4194320 | tf_op jit(solution)/shard_map/psum | solution.py:83
  513.2 3.0 divide_convert_fusion
  516.3 0.4 copy-done
  516.7 2.1 fusion.37
  518.8 13.9 %reduce-scatter.2.cloned.1.call-done = f32[128,512]{1,0:T(8,128)} async-done(((f32[256,512]{1,0:T(8,128)}), f32[128,512]{1,0:T(8,128)}) %reduce-scatter.2.cloned.1.call-update) | async-done | bytes 262160 | tf_op jit(solution)/shard_map/reduce_scatter | solution.py:90
  532.7 1.6 convert_element_type.23
  (93 shorter events, 4.4 us)
Async XLA Ops:
  6.5 47.2 %all-gather.2.cloned.1.call-start = ((), (), s32[]{:S(2)}) async-start(), calls=%async_computation.1 | async-start | bytes 2228224 | tf_op jit(solution)/shard_map/all_gather | solution.py:59
  7.3 506.0 %all-reduce.2.cloned.1.call-start = ((), (), s32[]{:S(2)}) async-start(), calls=%async_computation.2 | async-start | bytes 8388608 | tf_op jit(solution)/shard_map/psum | solution.py:83
  404.2 128.4 %reduce-scatter.2.cloned.1.call-start = ((), (), s32[]{:S(2)}) async-start(), calls=%async_computation.3 | async-start | bytes 786432 | tf_op jit(solution)/shard_map/reduce_scatter | solution.py:90
  513.2 3.4 copy-start
Sparse Core Ops, SparseCore 0:
  9.5 44.1 all-gather.1
  404.4 108.8 all-reduce.1
  518.9 13.7 reduce-scatter.1
where the time goes:
time: 541 us
  local copies, waits for them, and re-layouts  154 us (28%)
  matrix products  127 us (23%)
  blocking collectives  124 us (23%)
  waiting for transfers between devices  97.3 us (18%)
  other arithmetic  24.8 us (5%)
  between operations  13.2 us (2%)
    gather x4, local copies, waits for them, and re-layouts, weigh_block(): values = value_pages[index]  68.4 us
    gather x4, local copies, waits for them, and re-layouts, block_scores(): keys = key_pages[index]  68.4 us
    pmax x1, blocking collectives, shards(): largest = lax.pmax(maxima, 'seq')  64.9 us
    dot_general x4, matrix products, block_scores(): jnp.einsum('skgd,scktd->skgct', grouped, keys, preferred_element_type=jnp...  63.9 us
    dot_general x4, matrix products, weigh_block(): jnp.einsum('skgct,scktd->skgd', weights.astype(jnp.bfloat16), values, pre...  60.8 us
    psum x1, blocking collectives, shards(): summed_outputs, summed_totals = lax.psum((outputs, totals), 'seq')  58.7 us
    psum x1, waiting for transfers between devices, shards(): summed_outputs, summed_totals = lax.psum((outputs, totals), 'seq')  49.9 us
    all_gather x1, waiting for transfers between devices, shards(): all_queries = lax.all_gather(queries, 'seq', axis=0, tiled=True)  32.8 us
  transfers between devices with their start and end apart: 3, of which 3 were waited for; matrix products, arithmetic and copies ran while one was open for 3% of the time, Pallas kernels for 0%

commit v1 on v0

--- a/solution.py
+++ b/solution.py
@@ -56,7 +56,12 @@
         )
         return (totals, update)
 
-    all_queries = lax.all_gather(queries, "seq", axis=0, tiled=True)
+    ring = [queries]
+    for hop in range(15):
+        ring.append(lax.ppermute(ring[-1], "seq", [(dev, (dev + 1) % 16) for dev in range(16)]))
+    all_queries = jnp.roll(
+        jnp.concatenate(ring[::-1], axis=0), (lax.axis_index("seq") + 1) * ring[0].shape[0], axis=0
+    )
     batch_rows = all_queries.shape[0]
     block_size = math.gcd(batch_rows, 64)
     blocks = batch_rows // block_size

time: 541 us -> 611 us (1.13)
  waiting for transfers between devices: 97.3 us -> 164 us
    ppermute x0 -> x15, waiting for transfers between devices: none -> 100 us  [shards(): lax.ppermute(ring[-1], 'seq', [(dev, (dev + 1) % 16) for dev in range(16)])]
    all_gather x1 -> x0, waiting for transfers between devices: 32.8 us -> none  [shards(): all_queries = lax.all_gather(queries, 'seq', axis=0, tiled=True)]
  transfers between devices with their start and end apart: 3 -> 17, of which waited for: 3 -> 16; matrix products, arithmetic and copies ran while one was open for 3% -> 2% of each run, Pallas kernels for 0% -> 0%
where the time goes in v1:
time: 611 us; the launch traced here: 610 us
  waiting for transfers between devices  164 us (27%)
  local copies, waits for them, and re-layouts  154 us (25%)
  matrix products  126 us (21%)
  blocking collectives  126 us (21%)
  other arithmetic  24.8 us (4%)
  between operations  13.8 us (2%)
    ppermute x15, waiting for transfers between devices, shards(): lax.ppermute(ring[-1], 'seq', [(dev, (dev + 1) % 16) for dev in range(16)])  100 us
    gather x4, local copies, waits for them, and re-layouts, block_scores(): keys = key_pages[index]  68.5 us
    gather x4, local copies, waits for them, and re-layouts, weigh_block(): values = value_pages[index]  68.5 us
    pmax x1, blocking collectives, shards(): largest = lax.pmax(maxima, 'seq')  67.3 us
    dot_general x4, matrix products, block_scores(): jnp.einsum('skgd,scktd->skgct', grouped, keys, preferred_element_type=jnp...  62.9 us
    dot_general x4, matrix products, weigh_block(): jnp.einsum('skgct,scktd->skgd', weights.astype(jnp.bfloat16), values, pre...  60.7 us
    psum x1, blocking collectives, shards(): summed_outputs, summed_totals = lax.psum((outputs, totals), 'seq')  58.9 us
    psum x1, waiting for transfers between devices, shards(): summed_outputs, summed_totals = lax.psum((outputs, totals), 'seq')  50.1 us
  transfers between devices with their start and end apart: 17, of which 16 were waited for; matrix products, arithmetic and copies ran while one was open for 2% of the time, Pallas kernels for 0%

profile of v1, /device:TPU:0, one launch (start us, length us, event | category | flops | bytes accessed | tf_op | source)
XLA Modules:
  0.0 610.1 jit_solution(704367463531768662)
XLA Ops:
  7.0 7.8 %collective-permute-done = bf16[16,32,128]{2,1,0:T(8,128)(2,1)S(1)} collective-permute-done((bf16[16,32,128]{2,1,0:T(8,128)(2,1)}, bf16[16,32,128]{2,1,0:T(8,128)(2,1)S(1)}, u32[]{:S(2)}, u32[]{:S(2)}) %collective-permute-start) | collective-permute-done | bytes 131104 | tf_op jit(solution)/shard_map/ppermute | solution.py:61
  14.9 7.1 %collective-permute-done.1 = bf16[16,32,128]{2,1,0:T(8,128)(2,1)S(1)} collective-permute-done((bf16[16,32,128]{2,1,0:T(8,128)(2,1)S(1)}, bf16[16,32,128]{2,1,0:T(8,128)(2,1)S(1)}, u32[]{:S(2)}, u32[]{:S(2)}) %collective-permute-start.1) | collective-permute-done | bytes 131104 | tf_op jit(solution)/shard_map/ppermute | solution.py:61
  22.0 7.1 %collective-permute-done.2 = bf16[16,32,128]{2,1,0:T(8,128)(2,1)S(1)} collective-permute-done((bf16[16,32,128]{2,1,0:T(8,128)(2,1)S(1)}, bf16[16,32,128]{2,1,0:T(8,128)(2,1)S(1)}, u32[]{:S(2)}, u32[]{:S(2)}) %collective-permute-start.2) | collective-permute-done | bytes 131104 | tf_op jit(solution)/shard_map/ppermute | solution.py:61
  29.1 7.1 %collective-permute-done.3 = bf16[16,32,128]{2,1,0:T(8,128)(2,1)S(1)} collective-permute-done((bf16[16,32,128]{2,1,0:T(8,128)(2,1)S(1)}, bf16[16,32,128]{2,1,0:T(8,128)(2,1)S(1)}, u32[]{:S(2)}, u32[]{:S(2)}) %collective-permute-start.3) | collective-permute-done | bytes 131104 | tf_op jit(solution)/shard_map/ppermute | solution.py:61
  36.1 7.1 %collective-permute-done.4 = bf16[16,32,128]{2,1,0:T(8,128)(2,1)S(1)} collective-permute-done((bf16[16,32,128]{2,1,0:T(8,128)(2,1)S(1)}, bf16[16,32,128]{2,1,0:T(8,128)(2,1)S(1)}, u32[]{:S(2)}, u32[]{:S(2)}) %collective-permute-start.4) | collective-permute-done | bytes 131104 | tf_op jit(solution)/shard_map/ppermute | solution.py:61
  43.2 7.1 %collective-permute-done.5 = bf16[16,32,128]{2,1,0:T(8,128)(2,1)S(1)} collective-permute-done((bf16[16,32,128]{2,1,0:T(8,128)(2,1)S(1)}, bf16[16,32,128]{2,1,0:T(8,128)(2,1)S(1)}, u32[]{:S(2)}, u32[]{:S(2)}) %collective-permute-start.5) | collective-permute-done | bytes 131104 | tf_op jit(solution)/shard_map/ppermute | solution.py:61
  50.3 7.1 %collective-permute-done.6 = bf16[16,32,128]{2,1,0:T(8,128)(2,1)S(1)} collective-permute-done((bf16[16,32,128]{2,1,0:T(8,128)(2,1)S(1)}, bf16[16,32,128]{2,1,0:T(8,128)(2,1)S(1)}, u32[]{:S(2)}, u32[]{:S(2)}) %collective-permute-start.6) | collective-permute-done | bytes 131104 | tf_op jit(solution)/shard_map/ppermute | solution.py:61
  57.4 7.1 %collective-permute-done.7 = bf16[16,32,128]{2,1,0:T(8,128)(2,1)S(1)} collective-permute-done((bf16[16,32,128]{2,1,0:T(8,128)(2,1)S(1)}, bf16[16,32,128]{2,1,0:T(8,128)(2,1)S(1)}, u32[]{:S(2)}, u32[]{:S(2)}) %collective-permute-start.7) | collective-permute-done | bytes 131104 | tf_op jit(solution)/shard_map/ppermute | solution.py:61
  64.5 7.1 %collective-permute-done.8 = bf16[16,32,128]{2,1,0:T(8,128)(2,1)S(1)} collective-permute-done((bf16[16,32,128]{2,1,0:T(8,128)(2,1)S(1)}, bf16[16,32,128]{2,1,0:T(8,128)(2,1)S(1)}, u32[]{:S(2)}, u32[]{:S(2)}) %collective-permute-start.8) | collective-permute-done | bytes 131104 | tf_op jit(solution)/shard_map/ppermute | solution.py:61
  71.6 7.1 %collective-permute-done.9 = bf16[16,32,128]{2,1,0:T(8,128)(2,1)S(1)} collective-permute-done((bf16[16,32,128]{2,1,0:T(8,128)(2,1)S(1)}, bf16[16,32,128]{2,1,0:T(8,128)(2,1)S(1)}, u32[]{:S(2)}, u32[]{:S(2)}) %collective-permute-start.9) | collective-permute-done | bytes 131104 | tf_op jit(solution)/shard_map/ppermute | solution.py:61
  78.7 7.1 %collective-permute-done.10 = bf16[16,32,128]{2,1,0:T(8,128)(2,1)S(1)} collective-permute-done((bf16[16,32,128]{2,1,0:T(8,128)(2,1)S(1)}, bf16[16,32,128]{2,1,0:T(8,128)(2,1)S(1)}, u32[]{:S(2)}, u32[]{:S(2)}) %collective-permute-start.10) | collective-permute-done | bytes 131104 | tf_op jit(solution)/shard_map/ppermute | solution.py:61
  85.8 7.1 %collective-permute-done.11 = bf16[16,32,128]{2,1,0:T(8,128)(2,1)S(1)} collective-permute-done((bf16[16,32,128]{2,1,0:T(8,128)(2,1)S(1)}, bf16[16,32,128]{2,1,0:T(8,128)(2,1)S(1)}, u32[]{:S(2)}, u32[]{:S(2)}) %collective-permute-start.11) | collective-permute-done | bytes 131104 | tf_op jit(solution)/shard_map/ppermute | solution.py:61
  92.9 7.1 %collective-permute-done.12 = bf16[16,32,128]{2,1,0:T(8,128)(2,1)S(1)} collective-permute-done((bf16[16,32,128]{2,1,0:T(8,128)(2,1)S(1)}, bf16[16,32,128]{2,1,0:T(8,128)(2,1)S(1)}, u32[]{:S(2)}, u32[]{:S(2)}) %collective-permute-start.12) | collective-permute-done | bytes 131104 | tf_op jit(solution)/shard_map/ppermute | solution.py:61
  100.0 7.1 %collective-permute-done.13 = bf16[16,32,128]{2,1,0:T(8,128)(2,1)S(1)} collective-permute-done((bf16[16,32,128]{2,1,0:T(8,128)(2,1)S(1)}, bf16[16,32,128]{2,1,0:T(8,128)(2,1)S(1)}, u32[]{:S(2)}, u32[]{:S(2)}) %collective-permute-start.13) | collective-permute-done | bytes 131104 | tf_op jit(solution)/shard_map/ppermute | solution.py:61
  107.1 11.9 %slice_bitcast_fusion = (bf16[64,4,128,128]{3,2,1,0:T(8,128)(2,1)}, bf16[64,4,128,128]{3,2,1,0:T(8,128)(2,1)}) fusion(bf16[2,64,4,128,128]{4,3,2,1,0:T(8,128)(2,1)} %param.10), kind=kLoop, calls=%fused_computation.56 | loop fusion | bytes 33554432 | tf_op jit(solution)/shard_map/squeeze | solution.py:13
  120.7 141.4 %while.31 = (s32[]{:T(128)}, f32[4,64,4,8,4,128]{5,3,4,2,1,0:T(8,128)}, s32[4,64,4]{1,2,0:T(4,128)S(1)}, pred[4,64,4]{1,2,0:T(4,128)(4,1)S(1)}, f32[4,64,4,8]{3,...) while((s32[]{:T(128)}, ...), condition=%wide.region_4.5_spmd, body=%wide.region_0.4_spmd.sunk | while | flops 274403584 | bytes 114185880 | solution.py:78
  121.5 17.1 %gather_fusion.1 = bf16[256,4,128,128]{3,2,1,0:T(8,128)(2,1)} fusion(bf16[64,4,128,128]{3,2,1,0:T(8,128)(2,1)} %get-tuple-element.437, s32[1024]{0:T(1024)S(1)} %pad_clamp_fusion.4), kind=kCustom, calls=%fused_computation.clone.1 | custom fusion | bytes 67109888 | tf_op jit(solution)/shard_map/while/body/eval_jaxpr/gather | solution.py:38
  138.7 15.7 %bitcast_dynamic-update-slice_fusion.8 = (f32[4,64,4,8,4,128]{5,3,4,2,1,0:T(8,128)}, f32[64,4,8,4,128]{4,2,3,1,0:T(8,128)S(1)}) fusion(f32[4,64,4,8,4,128]{5,3,4,2,1,0:T(8,128)} %get-tuple-element.416, s32[]{:T(128)} %get-tuple-element.415, pred[64,4]{1,0:T(8,128)(4,1)S(1)} %copy.58, bf16[64,4,4,128,128]{4,3,2,1,0:T(8,128)(2,1)} %bitcast.114, ...), kind=kOutput, calls=%fused_computation.4.clone.1 | convolution fusion | flops 270532608 | bytes 42476544 | tf_op jit(solution)/shard_map/while/body/eval_jaxpr/skgd,scktd->skgct/dot_general | solution.py:40
  154.5 1.5 fusion.59
  156.9 17.1 %gather_fusion.1 = bf16[256,4,128,128]{3,2,1,0:T(8,128)(2,1)} fusion(bf16[64,4,128,128]{3,2,1,0:T(8,128)(2,1)} %get-tuple-element.437, s32[1024]{0:T(1024)S(1)} %pad_clamp_fusion.4), kind=kCustom, calls=%fused_computation.clone.1 | custom fusion | bytes 67109888 | tf_op jit(solution)/shard_map/while/body/eval_jaxpr/gather | solution.py:38
  174.1 15.7 %bitcast_dynamic-update-slice_fusion.8 = (f32[4,64,4,8,4,128]{5,3,4,2,1,0:T(8,128)}, f32[64,4,8,4,128]{4,2,3,1,0:T(8,128)S(1)}) fusion(f32[4,64,4,8,4,128]{5,3,4,2,1,0:T(8,128)} %get-tuple-element.416, s32[]{:T(128)} %get-tuple-element.415, pred[64,4]{1,0:T(8,128)(4,1)S(1)} %copy.58, bf16[64,4,4,128,128]{4,3,2,1,0:T(8,128)(2,1)} %bitcast.114, ...), kind=kOutput, calls=%fused_computation.4.clone.1 | convolution fusion | flops 270532608 | bytes 42476544 | tf_op jit(solution)/shard_map/while/body/eval_jaxpr/skgd,scktd->skgct/dot_general | solution.py:40
  189.8 1.5 fusion.59
  192.2 17.1 %gather_fusion.1 = bf16[256,4,128,128]{3,2,1,0:T(8,128)(2,1)} fusion(bf16[64,4,128,128]{3,2,1,0:T(8,128)(2,1)} %get-tuple-element.437, s32[1024]{0:T(1024)S(1)} %pad_clamp_fusion.4), kind=kCustom, calls=%fused_computation.clone.1 | custom fusion | bytes 67109888 | tf_op jit(solution)/shard_map/while/body/eval_jaxpr/gather | solution.py:38
  209.5 15.7 %bitcast_dynamic-update-slice_fusion.8 = (f32[4,64,4,8,4,128]{5,3,4,2,1,0:T(8,128)}, f32[64,4,8,4,128]{4,2,3,1,0:T(8,128)S(1)}) fusion(f32[4,64,4,8,4,128]{5,3,4,2,1,0:T(8,128)} %get-tuple-element.416, s32[]{:T(128)} %get-tuple-element.415, pred[64,4]{1,0:T(8,128)(4,1)S(1)} %copy.58, bf16[64,4,4,128,128]{4,3,2,1,0:T(8,128)(2,1)} %bitcast.114, ...), kind=kOutput, calls=%fused_computation.4.clone.1 | convolution fusion | flops 270532608 | bytes 42476544 | tf_op jit(solution)/shard_map/while/body/eval_jaxpr/skgd,scktd->skgct/dot_general | solution.py:40
  225.2 1.5 fusion.59
  227.6 17.1 %gather_fusion.1 = bf16[256,4,128,128]{3,2,1,0:T(8,128)(2,1)} fusion(bf16[64,4,128,128]{3,2,1,0:T(8,128)(2,1)} %get-tuple-element.437, s32[1024]{0:T(1024)S(1)} %pad_clamp_fusion.4), kind=kCustom, calls=%fused_computation.clone.1 | custom fusion | bytes 67109888 | tf_op jit(solution)/shard_map/while/body/eval_jaxpr/gather | solution.py:38
  244.8 15.7 %bitcast_dynamic-update-slice_fusion.8 = (f32[4,64,4,8,4,128]{5,3,4,2,1,0:T(8,128)}, f32[64,4,8,4,128]{4,2,3,1,0:T(8,128)S(1)}) fusion(f32[4,64,4,8,4,128]{5,3,4,2,1,0:T(8,128)} %get-tuple-element.416, s32[]{:T(128)} %get-tuple-element.415, pred[64,4]{1,0:T(8,128)(4,1)S(1)} %copy.58, bf16[64,4,4,128,128]{4,3,2,1,0:T(8,128)(2,1)} %bitcast.114, ...), kind=kOutput, calls=%fused_computation.4.clone.1 | convolution fusion | flops 270532608 | bytes 42476544 | tf_op jit(solution)/shard_map/while/body/eval_jaxpr/skgd,scktd->skgct/dot_general | solution.py:40
  260.5 1.5 fusion.59
  262.2 67.3 %pmax.7 = f32[4,64,4,8]{3,2,1,0:T(4,128)S(1)} all-reduce(f32[4,64,4,8]{3,2,1,0:T(4,128)S(1)} %get-tuple-element.215), channel_id=1, replica_groups=mesh['seq'=16,'head'=2] {'seq'}, use_global_device_ids=true, to_apply=%region_5.6 | all-reduce | flops 8192 | bytes 65536 | tf_op jit(solution)/shard_map/pmax | solution.py:79
  329.6 143.2 %while.32 = (s32[]{:T(128)}, f32[4,64,4,8]{3,2,1,0:T(4,128)S(1)}, f32[4,64,4,8,128]{4,3,2,1,0:T(8,128)}, pred[4,64,4]{1,2,0:T(4,128)(4,1)S(1)}, f32[4,64,4,8,4,1...) while((s32[]{:T(128)}, f32[4,64,4,8]{3,2,1,0:T(4,128)S(1)}, ...), condition=%wide.region_8.9_spmd, body=%wide.region_6.8_spmd.sunk | while | flops 274726656 | bytes 110420592 | solution.py:85
  329.8 17.1 %gather_fusion = bf16[256,4,128,128]{3,2,1,0:T(8,128)(2,1)} fusion(bf16[64,4,128,128]{3,2,1,0:T(8,128)(2,1)} %get-tuple-element.464, s32[1024]{0:T(1024)S(1)} %pad_clamp_fusion.5), kind=kCustom, calls=%fused_computation.1.clone.1 | custom fusion | bytes 67109888 | tf_op jit(solution)/shard_map/while/body/eval_jaxpr/gather | solution.py:50
  347.1 15.2 %fusion.63 = f32[4,64,4,8,128]{4,3,2,1,0:T(8,128)} fusion(f32[4,64,4,8,128]{4,3,2,1,0:T(8,128)} %get-tuple-element.450, s32[]{:T(128)} %get-tuple-element.448, bf16[64,4,4,128,128]{4,3,2,1,0:T(8,128)(2,1)} %bitcast.115, f32[4,64,4,8,4,128]{5,3,4,2,1,0:T(8,128)} %get-tuple-element.461, f32[64,4,8]{2,1,0:T(4,128)S(1)} %dynamic-slice_bitcast_fusion.4, ...), kind=kOutput, calls=%fused_computation.47.clone.1 | convolution fusion | flops 271581184 | bytes 38806784 | tf_op jit(solution)/shard_map/while/body/eval_jaxpr/skgct,scktd->skgd/dot_general | solution.py:51
  362.2 3.1 fusion.62
  365.6 17.1 %gather_fusion = bf16[256,4,128,128]{3,2,1,0:T(8,128)(2,1)} fusion(bf16[64,4,128,128]{3,2,1,0:T(8,128)(2,1)} %get-tuple-element.464, s32[1024]{0:T(1024)S(1)} %pad_clamp_fusion.5), kind=kCustom, calls=%fused_computation.1.clone.1 | custom fusion | bytes 67109888 | tf_op jit(solution)/shard_map/while/body/eval_jaxpr/gather | solution.py:50
  382.8 15.2 %fusion.63 = f32[4,64,4,8,128]{4,3,2,1,0:T(8,128)} fusion(f32[4,64,4,8,128]{4,3,2,1,0:T(8,128)} %get-tuple-element.450, s32[]{:T(128)} %get-tuple-element.448, bf16[64,4,4,128,128]{4,3,2,1,0:T(8,128)(2,1)} %bitcast.115, f32[4,64,4,8,4,128]{5,3,4,2,1,0:T(8,128)} %get-tuple-element.461, f32[64,4,8]{2,1,0:T(4,128)S(1)} %dynamic-slice_bitcast_fusion.4, ...), kind=kOutput, calls=%fused_computation.47.clone.1 | convolution fusion | flops 271581184 | bytes 38806784 | tf_op jit(solution)/shard_map/while/body/eval_jaxpr/skgct,scktd->skgd/dot_general | solution.py:51
  398.0 3.1 fusion.62
  401.4 17.1 %gather_fusion = bf16[256,4,128,128]{3,2,1,0:T(8,128)(2,1)} fusion(bf16[64,4,128,128]{3,2,1,0:T(8,128)(2,1)} %get-tuple-element.464, s32[1024]{0:T(1024)S(1)} %pad_clamp_fusion.5), kind=kCustom, calls=%fused_computation.1.clone.1 | custom fusion | bytes 67109888 | tf_op jit(solution)/shard_map/while/body/eval_jaxpr/gather | solution.py:50
  418.7 15.2 %fusion.63 = f32[4,64,4,8,128]{4,3,2,1,0:T(8,128)} fusion(f32[4,64,4,8,128]{4,3,2,1,0:T(8,128)} %get-tuple-element.450, s32[]{:T(128)} %get-tuple-element.448, bf16[64,4,4,128,128]{4,3,2,1,0:T(8,128)(2,1)} %bitcast.115, f32[4,64,4,8,4,128]{5,3,4,2,1,0:T(8,128)} %get-tuple-element.461, f32[64,4,8]{2,1,0:T(4,128)S(1)} %dynamic-slice_bitcast_fusion.4, ...), kind=kOutput, calls=%fused_computation.47.clone.1 | convolution fusion | flops 271581184 | bytes 38806784 | tf_op jit(solution)/shard_map/while/body/eval_jaxpr/skgct,scktd->skgd/dot_general | solution.py:51
  433.9 3.1 fusion.62
  437.2 17.1 %gather_fusion = bf16[256,4,128,128]{3,2,1,0:T(8,128)(2,1)} fusion(bf16[64,4,128,128]{3,2,1,0:T(8,128)(2,1)} %get-tuple-element.464, s32[1024]{0:T(1024)S(1)} %pad_clamp_fusion.5), kind=kCustom, calls=%fused_computation.1.clone.1 | custom fusion | bytes 67109888 | tf_op jit(solution)/shard_map/while/body/eval_jaxpr/gather | solution.py:50
  454.5 15.2 %fusion.63 = f32[4,64,4,8,128]{4,3,2,1,0:T(8,128)} fusion(f32[4,64,4,8,128]{4,3,2,1,0:T(8,128)} %get-tuple-element.450, s32[]{:T(128)} %get-tuple-element.448, bf16[64,4,4,128,128]{4,3,2,1,0:T(8,128)(2,1)} %bitcast.115, f32[4,64,4,8,4,128]{5,3,4,2,1,0:T(8,128)} %get-tuple-element.461, f32[64,4,8]{2,1,0:T(4,128)S(1)} %dynamic-slice_bitcast_fusion.4, ...), kind=kOutput, calls=%fused_computation.47.clone.1 | convolution fusion | flops 271581184 | bytes 38806784 | tf_op jit(solution)/shard_map/while/body/eval_jaxpr/skgct,scktd->skgd/dot_general | solution.py:51
  469.6 3.1 fusion.62
  473.0 58.9 %psum.15 = f32[256,4,8]{0,2,1:T(8,128)S(1)} all-reduce(f32[256,4,8]{0,2,1:T(8,128)S(1)} %copy.33), channel_id=1, replica_groups=mesh['seq'=16,'head'=2] {'seq'}, use_global_device_ids=true, to_apply=%region_10.11 | all-reduce | flops 8192 | bytes 65536 | tf_op jit(solution)/shard_map/psum | solution.py:88
  532.1 50.1 %all-reduce.2.cloned.1.call-done = f32[256,4,8,128]{3,2,1,0:T(8,128)} async-done(((f32[256,4,8,128]{3,2,1,0:T(8,128)}), f32[256,4,8,128]{3,2,1,0:T(8,128)}) %all-reduce.2.cloned.1.call-update) | async-done | bytes 4194320 | tf_op jit(solution)/shard_map/psum | solution.py:88
  582.2 3.0 divide_convert_fusion
  585.7 2.1 fusion.37
  587.8 13.9 %reduce-scatter.2.cloned.1.call-done = f32[128,512]{1,0:T(8,128)} async-done(((f32[256,512]{1,0:T(8,128)}), f32[128,512]{1,0:T(8,128)}) %reduce-scatter.2.cloned.1.call-update) | async-done | bytes 262160 | tf_op jit(solution)/shard_map/reduce_scatter | solution.py:95
  601.7 1.6 convert_element_type.23
  (159 shorter events, 8.2 us)
Async XLA Ops:
  6.5 112.4 %copy-start.1 = (s32[256,64]{0,1:T(8,128)S(1)}, s32[256,64]{0,1:T(8,128)}, u32[]{:S(2)}) copy-start(s32[256,64]{0,1:T(8,128)} %param.11) | copy-start | bytes 196612
  6.5 112.5 %copy-start.2 = (s32[256]{0:T(256)S(1)}, s32[256]{0:T(256)}, u32[]{:S(2)}) copy-start(s32[256]{0:T(256)} %param.12) | copy-start | bytes 3076
  6.5 575.7 %all-reduce.2.cloned.1.call-start = ((), (), s32[]{:S(2)}) async-start(), calls=%async_computation.1 | async-start | bytes 8388608 | tf_op jit(solution)/shard_map/psum | solution.py:88
  6.5 8.3 %collective-permute-start = (bf16[16,32,128]{2,1,0:T(8,128)(2,1)}, bf16[16,32,128]{2,1,0:T(8,128)(2,1)S(1)}, u32[]{:S(2)}, u32[]{:S(2)}) collective-permute-start(bf16[16,32,128]{2,1,0:T(8,128)(2,1)} %param.9), channel_id=1, source_target_pairs={{0,2},{2,4},{4,6},{6,8},{8,10},{10,12},{12,14},{14,16},{16,18},{18... | collective-permute-start | bytes 393224 | tf_op jit(solution)/shard_map/ppermute | solution.py:61
  14.9 7.1 %collective-permute-start.1 = (bf16[16,32,128]{2,1,0:T(8,128)(2,1)S(1)}, bf16[16,32,128]{2,1,0:T(8,128)(2,1)S(1)}, u32[]{:S(2)}, u32[]{:S(2)}) collective-permute-start(bf16[16,32,128]{2,1,0:T(8,128)(2,1)S(1)} %collective-permute-done), channel_id=1, source_target_pairs={{0,2},{2,4},{4,6},{6,8},{8,10},{10,12},{12,14},{14,16},{16,18},{18... | collective-permute-start | bytes 393224 | tf_op jit(solution)/shard_map/ppermute | solution.py:61
  22.0 7.1 %collective-permute-start.2 = (bf16[16,32,128]{2,1,0:T(8,128)(2,1)S(1)}, bf16[16,32,128]{2,1,0:T(8,128)(2,1)S(1)}, u32[]{:S(2)}, u32[]{:S(2)}) collective-permute-start(bf16[16,32,128]{2,1,0:T(8,128)(2,1)S(1)} %collective-permute-done.1), channel_id=1, source_target_pairs={{0,2},{2,4},{4,6},{6,8},{8,10},{10,12},{12,14},{14,16},{16,18},{18... | collective-permute-start | bytes 393224 | tf_op jit(solution)/shard_map/ppermute | solution.py:61
  29.1 7.1 %collective-permute-start.3 = (bf16[16,32,128]{2,1,0:T(8,128)(2,1)S(1)}, bf16[16,32,128]{2,1,0:T(8,128)(2,1)S(1)}, u32[]{:S(2)}, u32[]{:S(2)}) collective-permute-start(bf16[16,32,128]{2,1,0:T(8,128)(2,1)S(1)} %collective-permute-done.2), channel_id=1, source_target_pairs={{0,2},{2,4},{4,6},{6,8},{8,10},{10,12},{12,14},{14,16},{16,18},{18... | collective-permute-start | bytes 393224 | tf_op jit(solution)/shard_map/ppermute | solution.py:61
  36.1 7.1 %collective-permute-start.4 = (bf16[16,32,128]{2,1,0:T(8,128)(2,1)S(1)}, bf16[16,32,128]{2,1,0:T(8,128)(2,1)S(1)}, u32[]{:S(2)}, u32[]{:S(2)}) collective-permute-start(bf16[16,32,128]{2,1,0:T(8,128)(2,1)S(1)} %collective-permute-done.3), channel_id=1, source_target_pairs={{0,2},{2,4},{4,6},{6,8},{8,10},{10,12},{12,14},{14,16},{16,18},{18... | collective-permute-start | bytes 393224 | tf_op jit(solution)/shard_map/ppermute | solution.py:61
  43.2 7.1 %collective-permute-start.5 = (bf16[16,32,128]{2,1,0:T(8,128)(2,1)S(1)}, bf16[16,32,128]{2,1,0:T(8,128)(2,1)S(1)}, u32[]{:S(2)}, u32[]{:S(2)}) collective-permute-start(bf16[16,32,128]{2,1,0:T(8,128)(2,1)S(1)} %collective-permute-done.4), channel_id=1, source_target_pairs={{0,2},{2,4},{4,6},{6,8},{8,10},{10,12},{12,14},{14,16},{16,18},{18... | collective-permute-start | bytes 393224 | tf_op jit(solution)/shard_map/ppermute | solution.py:61
  50.3 7.1 %collective-permute-start.6 = (bf16[16,32,128]{2,1,0:T(8,128)(2,1)S(1)}, bf16[16,32,128]{2,1,0:T(8,128)(2,1)S(1)}, u32[]{:S(2)}, u32[]{:S(2)}) collective-permute-start(bf16[16,32,128]{2,1,0:T(8,128)(2,1)S(1)} %collective-permute-done.5), channel_id=1, source_target_pairs={{0,2},{2,4},{4,6},{6,8},{8,10},{10,12},{12,14},{14,16},{16,18},{18... | collective-permute-start | bytes 393224 | tf_op jit(solution)/shard_map/ppermute | solution.py:61
  57.4 7.1 %collective-permute-start.7 = (bf16[16,32,128]{2,1,0:T(8,128)(2,1)S(1)}, bf16[16,32,128]{2,1,0:T(8,128)(2,1)S(1)}, u32[]{:S(2)}, u32[]{:S(2)}) collective-permute-start(bf16[16,32,128]{2,1,0:T(8,128)(2,1)S(1)} %collective-permute-done.6), channel_id=1, source_target_pairs={{0,2},{2,4},{4,6},{6,8},{8,10},{10,12},{12,14},{14,16},{16,18},{18... | collective-permute-start | bytes 393224 | tf_op jit(solution)/shard_map/ppermute | solution.py:61
  64.5 7.1 %collective-permute-start.8 = (bf16[16,32,128]{2,1,0:T(8,128)(2,1)S(1)}, bf16[16,32,128]{2,1,0:T(8,128)(2,1)S(1)}, u32[]{:S(2)}, u32[]{:S(2)}) collective-permute-start(bf16[16,32,128]{2,1,0:T(8,128)(2,1)S(1)} %collective-permute-done.7), channel_id=1, source_target_pairs={{0,2},{2,4},{4,6},{6,8},{8,10},{10,12},{12,14},{14,16},{16,18},{18... | collective-permute-start | bytes 393224 | tf_op jit(solution)/shard_map/ppermute | solution.py:61
  71.6 7.1 %collective-permute-start.9 = (bf16[16,32,128]{2,1,0:T(8,128)(2,1)S(1)}, bf16[16,32,128]{2,1,0:T(8,128)(2,1)S(1)}, u32[]{:S(2)}, u32[]{:S(2)}) collective-permute-start(bf16[16,32,128]{2,1,0:T(8,128)(2,1)S(1)} %collective-permute-done.8), channel_id=1, source_target_pairs={{0,2},{2,4},{4,6},{6,8},{8,10},{10,12},{12,14},{14,16},{16,18},{18... | collective-permute-start | bytes 393224 | tf_op jit(solution)/shard_map/ppermute | solution.py:61
  78.7 7.1 %collective-permute-start.10 = (bf16[16,32,128]{2,1,0:T(8,128)(2,1)S(1)}, bf16[16,32,128]{2,1,0:T(8,128)(2,1)S(1)}, u32[]{:S(2)}, u32[]{:S(2)}) collective-permute-start(bf16[16,32,128]{2,1,0:T(8,128)(2,1)S(1)} %collective-permute-done.9), channel_id=1, source_target_pairs={{0,2},{2,4},{4,6},{6,8},{8,10},{10,12},{12,14},{14,16},{16,18},{18... | collective-permute-start | bytes 393224 | tf_op jit(solution)/shard_map/ppermute | solution.py:61
  85.8 7.1 %collective-permute-start.11 = (bf16[16,32,128]{2,1,0:T(8,128)(2,1)S(1)}, bf16[16,32,128]{2,1,0:T(8,128)(2,1)S(1)}, u32[]{:S(2)}, u32[]{:S(2)}) collective-permute-start(bf16[16,32,128]{2,1,0:T(8,128)(2,1)S(1)} %collective-permute-done.10), channel_id=1, source_target_pairs={{0,2},{2,4},{4,6},{6,8},{8,10},{10,12},{12,14},{14,16},{16,18},{18... | collective-permute-start | bytes 393224 | tf_op jit(solution)/shard_map/ppermute | solution.py:61
  92.9 7.1 %collective-permute-start.12 = (bf16[16,32,128]{2,1,0:T(8,128)(2,1)S(1)}, bf16[16,32,128]{2,1,0:T(8,128)(2,1)S(1)}, u32[]{:S(2)}, u32[]{:S(2)}) collective-permute-start(bf16[16,32,128]{2,1,0:T(8,128)(2,1)S(1)} %collective-permute-done.11), channel_id=1, source_target_pairs={{0,2},{2,4},{4,6},{6,8},{8,10},{10,12},{12,14},{14,16},{16,18},{18... | collective-permute-start | bytes 393224 | tf_op jit(solution)/shard_map/ppermute | solution.py:61
  100.0 7.1 %collective-permute-start.13 = (bf16[16,32,128]{2,1,0:T(8,128)(2,1)S(1)}, bf16[16,32,128]{2,1,0:T(8,128)(2,1)S(1)}, u32[]{:S(2)}, u32[]{:S(2)}) collective-permute-start(bf16[16,32,128]{2,1,0:T(8,128)(2,1)S(1)} %collective-permute-done.12), channel_id=1, source_target_pairs={{0,2},{2,4},{4,6},{6,8},{8,10},{10,12},{12,14},{14,16},{16,18},{18... | collective-permute-start | bytes 393224 | tf_op jit(solution)/shard_map/ppermute | solution.py:61
  107.1 12.1 %collective-permute-start.14 = (bf16[16,32,128]{2,1,0:T(8,128)(2,1)S(1)}, bf16[16,32,128]{2,1,0:T(8,128)(2,1)S(1)}, u32[]{:S(2)}, u32[]{:S(2)}) collective-permute-start(bf16[16,32,128]{2,1,0:T(8,128)(2,1)S(1)} %collective-permute-done.13), channel_id=1, source_target_pairs={{0,2},{2,4},{4,6},{6,8},{8,10},{10,12},{12,14},{14,16},{16,18},{18... | collective-permute-start | bytes 393224 | tf_op jit(solution)/shard_map/ppermute | solution.py:61
  118.9 0.9 copy-start
  472.8 128.9 %reduce-scatter.2.cloned.1.call-start = ((), (), s32[]{:S(2)}) async-start(), calls=%async_computation.2 | async-start | bytes 786432 | tf_op jit(solution)/shard_map/reduce_scatter | solution.py:95
  582.2 3.4 copy-start.3
Sparse Core Ops, SparseCore 0:
  472.9 109.3 all-reduce.1
  587.9 13.7 reduce-scatter.1
